TPU v7x, 32 devices: a whole 2x2x4 slice. The times are simulated.
32 devices in a mesh: tm: 8 (over z, y), freq: 4 (over x, core).
Axes of the slice: x: 2, y: 2, z: 4, core: 2. Of those that a mesh axis runs over, the one named last changes fastest.
Arguments:
- snapshots: bfloat16 [4352, 3, 4096], P('tm', None, 'freq'), may hold values from -200 to 200
- block_starts: int32 [32], replicated, may hold values from 0 to 4032, as said below
- freq_index: int32 [16], replicated, may hold values from 0 to 128
Outputs:
- modes: bfloat16 [16, 32, 2, 3, 4096], P(None, None, None, None, ('freq', 'tm'))
- energy: float32 [16], replicated
Inputs may be any that keep to these rules, and one draw needn't show every extreme that they name: `block_starts`: block b starts at b * 128 plus between 0 and 64.
All inputs are finite; a program needn't handle non-finite values.
Results may differ from a plain program's by a relative error of at most 0.0085.
Values may be sent and summed in bfloat16 or wider, within the bound.
A program may use at most 64 MiB of HBM per device.

v0:
```python
import math
import jax
import jax.numpy as jnp
from jax import lax
from jax.sharding import PartitionSpec as P

NB = 32
NFFT = 256
NF = 16
NSIT = 6


def for_sending(shard):
    return jax.tree.map(lambda a: a.astype(jnp.bfloat16) if a.dtype == jnp.float32 else a, shard)


def dft_rows(freq_index):
    times_idx = jnp.arange(NFFT, dtype=jnp.int32)
    phase_int = freq_index[:, None] * times_idx[None, :] % NFFT
    angles = 2.0 * math.pi / NFFT * phase_int.astype(jnp.float32)
    window = 0.5 - 0.5 * jnp.cos(2.0 * math.pi / NFFT * times_idx.astype(jnp.float32))
    scaling = 1.0 / jnp.sqrt(jnp.sum(window * window))
    cosine = window[None, :] * jnp.cos(angles) * scaling
    sine_rows = -window[None, :] * jnp.sin(angles) * scaling
    return jnp.stack([cosine, sine_rows], 1).reshape(2 * NF, NFFT).astype(jnp.bfloat16)


def block_rows(block_starts):
    return block_starts[:, None] + jnp.arange(NFFT, dtype=jnp.int32)[None, :]


def matmul_batch(left, right):
    return jnp.einsum("fij,fjk->fik", left, right, precision=lax.Precision.HIGHEST)


def whiten(summed, points):
    gram_re = summed[:, 0]
    gram_im = summed[:, 1]
    top_rows = jnp.concatenate([gram_re, -gram_im], 2)
    low_rows = jnp.concatenate([gram_im, gram_re], 2)
    hermit = jnp.concatenate([top_rows, low_rows], 1)
    frob = jnp.sqrt(jnp.sum(hermit * hermit, axis=(1, 2)) + 1e-06)
    identity = jnp.eye(2 * NB, dtype=jnp.float32)[None]
    iterate = hermit / frob[:, None, None]
    inverse = jnp.broadcast_to(identity, hermit.shape)
    for iteration in range(NSIT):
        factor = 1.5 * identity - 0.5 * matmul_batch(inverse, iterate)
        iterate = matmul_batch(iterate, factor)
        inverse = matmul_batch(factor, inverse)
    columns = inverse[:, :, :NB] * jnp.sqrt(6.0 * points / frob)[:, None, None]
    upper = columns[:, :NB]
    lower = columns[:, NB:]
    coefficients = jnp.stack([jnp.stack([upper, -lower], 1), jnp.stack([lower, upper], 1)], 1)
    energy = jnp.trace(gram_re, axis1=1, axis2=2) / (3.0 * NB * points)
    return (coefficients, energy)


def local(snapshots, block_starts, freq_index):
    dft_table = dft_rows(freq_index)
    offsets = block_rows(block_starts)
    series = lax.all_to_all(snapshots, "tm", split_axis=2, concat_axis=0, tiled=True)
    count = series.shape[1]
    width = series.shape[2]
    columns_all = series.reshape(series.shape[0], count * width)
    windows = jnp.take(columns_all, offsets, axis=0)
    spectra_part = jnp.einsum(
        "rt,btn->rbn", dft_table, windows, preferred_element_type=jnp.float32
    ).astype(jnp.bfloat16)
    spectra = spectra_part.reshape(2 * NF, NB, count, width)
    width = spectra.shape[3]
    points = float(width * lax.axis_size("tm") * lax.axis_size("freq"))
    flat_spec = spectra.reshape(NF, 2, NB, 3 * width)
    real_part = flat_spec[:, 0]
    imag_part = flat_spec[:, 1]
    gram_re = jnp.einsum("fbn,fcn->fbc", real_part, real_part, preferred_element_type=jnp.float32)
    gram_re = gram_re + jnp.einsum(
        "fbn,fcn->fbc", imag_part, imag_part, preferred_element_type=jnp.float32
    )
    cross_terms = jnp.einsum(
        "fbn,fcn->fbc", real_part, imag_part, preferred_element_type=jnp.float32
    )
    partial_gram = jnp.stack([gram_re, cross_terms - jnp.swapaxes(cross_terms, 1, 2)], 1)
    shared = lax.psum_scatter(partial_gram, "freq", scatter_dimension=0, tiled=True)
    shared = lax.psum(shared, "tm")
    coef_part, energy_part = whiten(shared, points)
    coefficients, energy = (
        lax.all_gather(for_sending(coef_part), "freq", axis=0, tiled=True).astype(coef_part.dtype),
        lax.all_gather(for_sending(energy_part), "freq", axis=0, tiled=True).astype(
            energy_part.dtype
        ),
    )
    coef_bf = jnp.transpose(coefficients.astype(jnp.bfloat16), (0, 4, 1, 2, 3))
    modes = jnp.einsum(
        "fjorb,frbn->fjon", coef_bf, flat_spec, preferred_element_type=jnp.float32
    ).astype(jnp.bfloat16)
    return (modes.reshape(NF, NB, 2, 3, width), energy)


def solution(mesh):
    return jax.shard_map(
        local,
        mesh=mesh,
        in_specs=(P("tm", None, "freq"), P(), P()),
        out_specs=(P(None, None, None, None, ("freq", "tm")), P()),
        check_vma=False,
    )
```

profile of v0, /device:TPU:0, one launch (start us, length us, event | category | flops | bytes accessed | tf_op | source)
XLA Modules:
  0.0 302.0 jit_solution(5454978820925684729)
XLA Ops:
  7.2 8.6 %copy.43 = bf16[544,3,1024]{0,1,2:T(4,128)(2,1)} copy(bf16[544,3,1024]{2,0,1:T(8,128)(2,1)} %param.3) | data formatting | bytes 6684672 | tf_op args[0]
  15.8 7.4 %all-to-all-start = ((bf16[544,3,1024]{0,1,2:T(4,128)(2,1)}), bf16[544,3,1024]{0,1,2:T(4,128)(2,1)}, u32[]{:S(2)}, u32[]{:S(2)}) async-start(bf16[544,3,1024]{0,1,2:T(4,128)(2,1)} %copy.43), calls=%async_computation | async-start | bytes 10485760 | tf_op jit(solution)/shard_map/all_to_all | solution.py:61
  23.3 0.6 multiply_reduce_fusion.1
  24.7 0.2 multiply_convert_fusion.1
  25.0 0.6 fusion.43
  27.1 111.9 %all-to-all-done = bf16[544,3,1024]{0,1,2:T(4,128)(2,1)} async-done(((bf16[544,3,1024]{0,1,2:T(4,128)(2,1)}), bf16[544,3,1024]{0,1,2:T(4,128)(2,1)}, u32[]{:S(2)}, u32[]{:S(2)}) %all-to-all-start) | async-done | bytes 3342368 | tf_op jit(solution)/shard_map/all_to_all | solution.py:61
  139.0 7.4 %copy.74 = bf16[544,3,8,128]{0,2,3,1:T(8,128)(2,1)} copy(bf16[544,3,8,128]{0,1,3,2:T(4,128)(2,1)} %bitcast) | data formatting | bytes 6684672 | tf_op jit(solution)/shard_map/all_to_all | solution.py:61
  146.4 7.4 %reshape.243 = bf16[4352,384]{0,1:T(8,128)(2,1)} reshape(bf16[8,544,3,128]{1,0,3,2:T(8,128)(2,1)} %bitcast.97) | data formatting | bytes 6684672 | tf_op jit(solution)/shard_map/reshape | solution.py:64
  153.7 5.6 %copy.45 = bf16[4352,384]{1,0:T(8,128)(2,1)S(1)} copy(bf16[4352,384]{0,1:T(8,128)(2,1)} %reshape.243) | data formatting | bytes 6684672 | tf_op jit(solution)/shard_map/reshape | solution.py:64
  159.4 33.1 %gather_fusion = bf16[8192,384]{1,0:T(8,128)(2,1)} fusion(bf16[4352,384]{1,0:T(8,128)(2,1)S(1)} %copy.45, s32[8192]{0:T(1024)S(1)} %broadcast_clamp_fusion), kind=kCustom, calls=%fused_computation | custom fusion | bytes 12615680 | tf_op jit(solution)/shard_map/jit(_take)/gather | solution.py:65
  192.5 4.6 %fusion.4 = bf16[32,32,384]{2,0,1:T(8,128)(2,1)S(1)} fusion(bf16[32,256,1]{1,0,2:T(8,128)(2,1)S(1)} %reshape.260, bf16[32,256,384]{2,1,0:T(8,128)(2,1)} %bitcast.99, pred[32,256]{1,0:T(8,128)(4,1)S(1)} %fusion.31), kind=kOutput, calls=%fused_computation.7 | convolution fusion | flops 204865536 | bytes 7102464 | tf_op jit(solution)/shard_map/rt,btn->rbn/dot_general | solution.py:66
  197.1 0.3 reshape_reshape.3
  197.4 1.1 fusion.42
  198.5 0.3 fusion.18
  198.8 0.5 fusion.17
  199.4 0.1 copy.48
  199.6 0.3 fusion.7
  199.9 0.8 pad_maximum_fusion
  200.8 32.6 %all-reduce.4.cloned.1.call-done = f32[16,2,32,32]{3,2,0,1:T(8,128)} async-done(((f32[16,2,32,32]{3,2,0,1:T(8,128)}), f32[16,2,32,32]{3,2,0,1:T(8,128)}) %all-reduce.4.cloned.1.call-update) | async-done | bytes 131088
  233.4 0.9 constant_dynamic-slice_fusion
  234.3 38.6 %psum.7 = f32[4,2,32,32]{3,2,0,1:T(8,128)S(1)} all-reduce(f32[4,2,32,32]{3,2,0,1:T(8,128)S(1)} %constant_dynamic-slice_fusion), channel_id=1, replica_groups=mesh['tm'=8,'freq'=4] {'tm'}, use_global_device_ids=true, to_apply=%region_2.3 | all-reduce | flops 8192 | bytes 65536 | tf_op jit(solution)/shard_map/psum | solution.py:84
  273.0 0.1 select_reduce_fusion
  273.1 0.2 multiply_reduce_fusion
  273.3 0.4 fusion.13
  273.7 0.3 fusion.41
  274.0 0.3 fusion.20
  274.2 0.3 fusion.12
  274.5 0.3 fusion.45
  274.8 0.3 fusion.44
  275.0 0.3 fusion.11
  275.3 0.3 fusion.47
  275.6 0.3 fusion.46
  275.8 0.3 fusion.10
  276.1 0.3 fusion.49
  276.3 0.3 fusion.48
  276.6 0.3 fusion.9
  276.9 0.3 fusion.51
  277.1 0.3 fusion.50
  277.4 0.3 fusion.8
  277.7 0.4 convolution_multiply_fusion.6
  278.1 0.1 fusion.24
  278.3 6.5 %all_gather.6 = bf16[16,2,2,32,32]{3,4,0,2,1:T(8,128)(2,1)S(1)} all-gather(bf16[4,2,2,32,32]{3,4,0,2,1:T(8,128)(2,1)S(1)} %pad_maximum_fusion.1), channel_id=1, replica_groups=mesh['tm'=8,'freq'=4] {'freq'}, dimensions={0}, use_global_device_ids=true | all-gather | bytes 163840 | tf_op jit(solution)/shard_map/all_gather | solution.py:87
  284.8 0.4 bitcast_convert_fusion
  285.2 0.3 reshape.244
  285.5 0.2 dynamic-update-slice
  285.8 2.1 copy.52
  287.9 6.8 %all-reduce = bf16[16]{0:T(256)(128)(2,1)S(1)} all-reduce(bf16[16]{0:T(256)(128)(2,1)S(1)} %dynamic-update-slice), channel_id=1, replica_groups=mesh['tm'=8,'freq'=4] {'freq'}, use_global_device_ids=true, to_apply=%add | all-reduce | flops 16 | bytes 64
  294.7 0.5 convert_element_type.64
  (27 shorter events, 0.6 us)
Async XLA Ops:
  15.8 8.9 %copy-start.2 = (s32[16]{0:T(128)S(1)}, s32[16]{0:T(128)}, u32[]{:S(2)}) copy-start(s32[16]{0:T(128)} %param.5) | copy-start | bytes 196
  15.8 9.1 %copy-start = (s32[32]{0:T(128)S(1)}, s32[32]{0:T(128)}, u32[]{:S(2)}) copy-start(s32[32]{0:T(128)} %param.4) | copy-start | bytes 388
  15.8 9.2 %copy-start.1 = (u32[32]{0:T(128)S(1)}, u32[32]{0:T(128)}, u32[]{:S(2)}) copy-start(u32[32]{0:T(128)} %constant.55) | copy-start | bytes 388
  15.8 123.2 %all-to-all-start = ((bf16[544,3,1024]{0,1,2:T(4,128)(2,1)}), bf16[544,3,1024]{0,1,2:T(4,128)(2,1)}, u32[]{:S(2)}, u32[]{:S(2)}) async-start(bf16[544,3,1024]{0,1,2:T(4,128)(2,1)} %copy.43), calls=%async_computation | async-start | bytes 10485760 | tf_op jit(solution)/shard_map/all_to_all | solution.py:61
  23.2 210.1 %all-reduce.4.cloned.1.call-start = ((), (), s32[]{:S(2)}) async-start(), calls=%async_computation.1 | async-start | bytes 1048576
Sparse Core Ops, SparseCore 0:
  200.9 32.4 all-reduce.3
where the time goes:
time: 303 us; the launch traced here: 302 us
  waiting for transfers between devices  145 us (48%)
  local copies, waits for them, and re-layouts  67.9 us (22%)
  blocking collectives  51.9 us (17%)
  between operations  16.4 us (5%)
  matrix products  10.8 us (4%)
  starting transfers between devices  7.49 us (2%)
    all_to_all x1, waiting for transfers between devices, local(): lax.all_to_all(snapshots, 'tm', split_axis=2, concat_axis=0, tiled=True)  112 us
    psum x1, blocking collectives, local(): shared = lax.psum(shared, 'tm')  38.6 us
    gather x1, local copies, waits for them, and re-layouts, local(): windows = jnp.take(columns_all, offsets, axis=0)  33.1 us
    unnamed x2, waiting for transfers between devices  32.6 us
    reshape x2, local copies, waits for them, and re-layouts, local(): columns_all = series.reshape(series.shape[0], count * width)  13 us
    unnamed x13, local copies, waits for them, and re-layouts  12.5 us
    all_to_all x1, starting transfers between devices, local(): lax.all_to_all(snapshots, 'tm', split_axis=2, concat_axis=0, tiled=True)  7.45 us
    all_to_all x1, local copies, waits for them, and re-layouts, local(): lax.all_to_all(snapshots, 'tm', split_axis=2, concat_axis=0, tiled=True)  7.37 us
  transfers between devices with their start and end apart: 2, of which 2 were waited for; matrix products, arithmetic and copies ran while one was open for 1% of the time, Pallas kernels for 0%

commit v1 on v0

--- a/solution.py
+++ b/solution.py
@@ -58,7 +58,10 @@
 def local(snapshots, block_starts, freq_index):
     dft_table = dft_rows(freq_index)
     offsets = block_rows(block_starts)
-    series = lax.all_to_all(snapshots, "tm", split_axis=2, concat_axis=0, tiled=True)
+    series = jnp.concatenate(
+        lax.all_to_all(jnp.stack(jnp.split(snapshots, lax.axis_size("tm"), axis=2)), "tm", 0, 0),
+        axis=0,
+    )
     count = series.shape[1]
     width = series.shape[2]
     columns_all = series.reshape(series.shape[0], count * width)

time: 303 us -> 250 us (0.83)
  waiting for transfers between devices: 145 us -> 104 us
  local copies, waits for them, and re-layouts: 67.9 us -> 56.1 us
    all_to_all x1, waiting for transfers between devices: 112 us -> 71.1 us  [local(): lax.all_to_all(jnp.stack(jnp.split(snapshots, lax.axis_size('tm'), axis=2...]
    reshape x2 -> x0, local copies, waits for them, and re-layouts: 13 us -> none  [local(): columns_all = series.reshape(series.shape[0], count * width)]
    all_to_all x1 -> x0, local copies, waits for them, and re-layouts: 7.37 us -> none  [local(): lax.all_to_all(snapshots, 'tm', split_axis=2, concat_axis=0, tiled=True)]
    unnamed x13 -> x20, local copies, waits for them, and re-layouts: 12.5 us -> 17 us
    another operation x0 -> x2, local copies, waits for them, and re-layouts: none -> 4.09 us  [the longest x1 2.29 us: local(): columns_all = series.reshape(series.shape[0], count * width)]
where the time goes in v1:
time: 250 us; the launch traced here: 249 us
  waiting for transfers between devices  104 us (42%)
  local copies, waits for them, and re-layouts  56.1 us (22%)
  blocking collectives  51.9 us (21%)
  between operations  16.4 us (7%)
  matrix products  10.8 us (4%)
  starting transfers between devices  7.48 us (3%)
  other arithmetic  2.93 us (1%)
    all_to_all x1, waiting for transfers between devices, local(): lax.all_to_all(jnp.stack(jnp.split(snapshots, lax.axis_size('tm'), axis=2...  71.1 us
    psum x1, blocking collectives, local(): shared = lax.psum(shared, 'tm')  38.4 us
    gather x1, local copies, waits for them, and re-layouts, local(): windows = jnp.take(columns_all, offsets, axis=0)  33.1 us
    unnamed x2, waiting for transfers between devices  32.6 us
    unnamed x20, local copies, waits for them, and re-layouts  17 us
    all_to_all x1, starting transfers between devices, local(): lax.all_to_all(jnp.stack(jnp.split(snapshots, lax.axis_size('tm'), axis=2...  7.44 us
    unnamed x1, blocking collectives  6.78 us
    all_gather x1, blocking collectives, local(): lax.all_gather(for_sending(coef_part), 'freq', axis=0, tiled=True)  6.68 us
  transfers between devices with their start and end apart: 2, of which 2 were waited for; matrix products, arithmetic and copies ran while one was open for 1% of the time, Pallas kernels for 0%

profile of v1, /device:TPU:0, one launch (start us, length us, event | category | flops | bytes accessed | tf_op | source)
XLA Modules:
  0.0 249.4 jit_solution(18214542786638048519)
XLA Ops:
  7.2 1.8 bitcast_dynamic-update-slice_fusion.7
  8.9 1.8 bitcast_dynamic-update-slice_fusion.6
  10.7 1.8 bitcast_dynamic-update-slice_fusion.5
  12.5 1.8 bitcast_dynamic-update-slice_fusion.4
  14.3 1.8 bitcast_dynamic-update-slice_fusion.3
  16.1 1.8 bitcast_dynamic-update-slice_fusion.2
  17.9 1.8 bitcast_dynamic-update-slice_fusion.1
  19.7 1.8 bitcast_dynamic-update-slice_fusion
  21.5 7.4 %all-to-all-start = ((bf16[8,544,3,128]{3,1,2,0:T(8,128)(2,1)}), bf16[8,544,3,128]{3,1,2,0:T(8,128)(2,1)S(1)}, u32[]{:S(2)}, u32[]{:S(2)}) async-start(bf16[8,544,3,128]{3,1,2,0:T(8,128)(2,1)} %bitcast_dynamic-update-slice_fusion), calls=%async_computation | async-start | bytes 6684672 | tf_op jit(solution)/shard_map/all_to_all | solution.py:62
  29.0 0.6 multiply_reduce_fusion.1
  30.8 0.6 fusion.43
  32.8 71.1 %all-to-all-done = bf16[8,544,3,128]{3,1,2,0:T(8,128)(2,1)S(1)} async-done(((bf16[8,544,3,128]{3,1,2,0:T(8,128)(2,1)}), bf16[8,544,3,128]{3,1,2,0:T(8,128)(2,1)S(1)}, u32[]{:S(2)}, u32[]{:S(2)}) %all-to-all-start) | async-done | bytes 3342368 | tf_op jit(solution)/shard_map/all_to_all | solution.py:62
  103.9 2.3 copy.53
  106.2 0.6 copy.74
  106.8 33.1 %gather_fusion = bf16[8192,384]{1,0:T(8,128)(2,1)} fusion(bf16[4352,384]{1,0:T(8,128)(2,1)S(1)} %bitcast.110, s32[8192]{0:T(1024)S(1)} %broadcast_clamp_fusion), kind=kCustom, calls=%fused_computation | custom fusion | bytes 12615680 | tf_op jit(solution)/shard_map/jit(_take)/gather | solution.py:68
  139.9 4.6 %fusion.4 = bf16[32,32,384]{2,0,1:T(8,128)(2,1)S(1)} fusion(bf16[32,256,1]{1,0,2:T(8,128)(2,1)S(1)} %reshape.255, bf16[32,256,384]{2,1,0:T(8,128)(2,1)} %bitcast.113, pred[32,256]{1,0:T(8,128)(4,1)S(1)} %fusion.31), kind=kOutput, calls=%fused_computation.7 | convolution fusion | flops 204865536 | bytes 7102464 | tf_op jit(solution)/shard_map/rt,btn->rbn/dot_general | solution.py:69
  144.5 0.3 reshape_reshape.7
  144.8 1.1 fusion.42
  145.9 0.3 fusion.18
  146.2 0.5 fusion.17
  146.9 0.3 fusion.7
  147.3 0.8 pad_maximum_fusion
  148.2 32.6 %all-reduce.4.cloned.1.call-done = f32[16,2,32,32]{3,2,0,1:T(8,128)} async-done(((f32[16,2,32,32]{3,2,0,1:T(8,128)}), f32[16,2,32,32]{3,2,0,1:T(8,128)}) %all-reduce.4.cloned.1.call-update) | async-done | bytes 131088
  180.8 0.9 constant_dynamic-slice_fusion
  181.7 38.4 %psum.7 = f32[4,2,32,32]{3,2,0,1:T(8,128)S(1)} all-reduce(f32[4,2,32,32]{3,2,0,1:T(8,128)S(1)} %constant_dynamic-slice_fusion), channel_id=1, replica_groups=mesh['tm'=8,'freq'=4] {'tm'}, use_global_device_ids=true, to_apply=%region_2.3 | all-reduce | flops 8192 | bytes 65536 | tf_op jit(solution)/shard_map/psum | solution.py:87
  220.5 0.4 fusion.13
  220.9 0.3 fusion.41
  221.2 0.3 fusion.20
  221.4 0.3 fusion.12
  221.7 0.3 fusion.45
  222.0 0.3 fusion.44
  222.2 0.3 fusion.11
  222.5 0.3 fusion.47
  222.8 0.3 fusion.46
  223.0 0.3 fusion.10
  223.3 0.3 fusion.49
  223.6 0.3 fusion.48
  223.8 0.3 fusion.9
  224.1 0.3 fusion.51
  224.3 0.3 fusion.50
  224.6 0.3 fusion.8
  224.9 0.4 convolution_multiply_fusion.6
  225.5 6.7 %all_gather.6 = bf16[16,2,2,32,32]{3,4,0,2,1:T(8,128)(2,1)S(1)} all-gather(bf16[4,2,2,32,32]{3,4,0,2,1:T(8,128)(2,1)S(1)} %pad_maximum_fusion.1), channel_id=1, replica_groups=mesh['tm'=8,'freq'=4] {'freq'}, dimensions={0}, use_global_device_ids=true | all-gather | bytes 163840 | tf_op jit(solution)/shard_map/all_gather | solution.py:90
  232.2 0.4 bitcast_convert_fusion
  232.6 0.3 reshape.239
  233.2 2.1 copy.49
  235.3 6.8 %all-reduce = bf16[16]{0:T(256)(128)(2,1)S(1)} all-reduce(bf16[16]{0:T(256)(128)(2,1)S(1)} %dynamic-update-slice), channel_id=1, replica_groups=mesh['tm'=8,'freq'=4] {'freq'}, use_global_device_ids=true, to_apply=%add | all-reduce | flops 16 | bytes 64
  242.0 0.5 convert_element_type.64
  (33 shorter events, 1.5 us)
Async XLA Ops:
  21.5 8.9 %copy-start.2 = (s32[16]{0:T(128)S(1)}, s32[16]{0:T(128)}, u32[]{:S(2)}) copy-start(s32[16]{0:T(128)} %param.5) | copy-start | bytes 196
  21.5 9.1 %copy-start = (s32[32]{0:T(128)S(1)}, s32[32]{0:T(128)}, u32[]{:S(2)}) copy-start(s32[32]{0:T(128)} %param.4) | copy-start | bytes 388
  21.5 9.2 %copy-start.1 = (u32[32]{0:T(128)S(1)}, u32[32]{0:T(128)}, u32[]{:S(2)}) copy-start(u32[32]{0:T(128)} %constant.55) | copy-start | bytes 388
  21.5 82.4 %all-to-all-start = ((bf16[8,544,3,128]{3,1,2,0:T(8,128)(2,1)}), bf16[8,544,3,128]{3,1,2,0:T(8,128)(2,1)S(1)}, u32[]{:S(2)}, u32[]{:S(2)}) async-start(bf16[8,544,3,128]{3,1,2,0:T(8,128)(2,1)} %bitcast_dynamic-update-slice_fusion), calls=%async_computation | async-start | bytes 6684672 | tf_op jit(solution)/shard_map/all_to_all | solution.py:62
  29.0 151.8 %all-reduce.4.cloned.1.call-start = ((), (), s32[]{:S(2)}) async-start(), calls=%async_computation.1 | async-start | bytes 1048576
Sparse Core Ops, SparseCore 0:
  148.3 32.4 all-reduce.3
